TPU v7x, 32 devices: a whole 2x2x4 slice. The times are simulated.
32 devices in a mesh: gene: 8 (over z, x), cell: 4 (over y, core).
Axes of the slice: x: 2, y: 2, z: 4, core: 2. Of those that a mesh axis runs over, the one named last changes fastest.
Arguments:
- pool_counts: bfloat16 [20480, 16384], P('gene', 'cell'), may hold values from 0 to 6.5
- cell_picks: int32 [7, 4096], P(None, 'cell'), may hold values from 0 to 16383, as said below
- loadings_init: float32 [64, 20480], P(None, 'gene'), may hold values from -0.0390625 to 0.0390625
Outputs:
- scaled_loadings: float32 [64, 20480], P(None, 'gene')
Inputs may be any that keep to these rules, and one draw needn't show every extreme that they name: `cell_picks`: column b of every row names a pool cell in [(b // 1024) * 4096, (b // 1024 + 1) * 4096); no cell is named twice in one row.
All inputs are finite; a program needn't handle non-finite values.
Results may differ from a plain program's by a relative error of at most 0.018.
Values may be sent and summed in bfloat16 or wider, within the bound.
A program may use at most 128 MiB of HBM per device.

v0:
```python
import functools
import math

import jax
import jax.numpy as jnp
from jax import lax
from jax.experimental import pallas as pl
from jax.experimental.pallas import tpu as pltpu
from jax.sharding import PartitionSpec as P

STEPS = 7
MESH = pl.DeviceIdType.MESH

step_rate = 1.0


def transposed_product(left, right):
    return lax.dot_general(
        left, right, (((1,), (1,)), ((), ())), preferred_element_type=jnp.float32
    )


def sum_kernel(axis, n, arrays, gather, *refs):
    inputs = refs[:arrays]
    refs = refs[arrays:]
    if gather:
        pool_ref, picks_ref = refs[:2]
        refs = refs[2:]
    outputs = refs[:arrays]
    refs = refs[arrays:]
    if gather:
        tile_ref = refs[0]
        refs = refs[1:]
    landed, reduced, whole = (refs[i * arrays:(i + 1) * arrays] for i in range(3))
    sends, arrivals, sends_back, arrivals_back = refs[3 * arrays:3 * arrays + 4]
    me = lax.axis_index(axis)
    barrier = pltpu.get_barrier_semaphore()
    peers = [lax.rem(me + k, n) for k in range(n)]
    for k in range(1, n):
        pl.semaphore_signal(barrier, inc=1, device_id={axis: peers[k]}, device_id_type=MESH)
    blocks = 0
    if gather:
        held, hot, loaded = refs[3 * arrays + 4:]
        start, block, blocks = gather
        loads = []
        for b in range(blocks):
            load = pltpu.make_async_copy(
                pool_ref.at[pl.ds(start + b * block, block)],
                held.at[pl.ds(b * block, block)],
                loaded.at[b],
            )
            load.start()
            loads.append(load)

    def select_columns(b):
        loads[b].wait()
        rows = pl.ds(b * block, block)
        width = min(512, hot.shape[1])

        def piece(j, carry):
            columns = pl.ds(pl.multiple_of(j * width, width), width)
            tile_ref[rows, columns] = jnp.dot(
                held[rows, :], hot[:, columns], preferred_element_type=jnp.float32
            ).astype(tile_ref.dtype)
            return carry

        lax.fori_loop(0, hot.shape[1] // width, piece, 0)

    pl.semaphore_wait(barrier, n - 1)
    copies = []
    for a in range(arrays):
        for k in range(1, n):
            copy = pltpu.make_async_remote_copy(
                src_ref=inputs[a].at[peers[k]],
                dst_ref=landed[a].at[k - 1],
                send_sem=sends.at[a, k - 1],
                recv_sem=arrivals.at[a, k - 1],
                device_id={axis: peers[k]},
                device_id_type=MESH,
            )
            copy.start()
            copies.append(copy)
    if gather:
        depth = 256

        def mark(i, carry):
            ids = lax.broadcasted_iota(jnp.int32, (depth, hot.shape[1]), 0) + i * depth
            hot[pl.ds(pl.multiple_of(i * depth, depth), depth), :] = jnp.where(
                ids == picks_ref[...], 1.0, 0.0
            ).astype(hot.dtype)
            return carry

        lax.fori_loop(0, hot.shape[0] // depth, mark, 0)
    early = blocks // 2
    for b in range(early):
        select_columns(b)
    for copy in copies:
        copy.wait_recv()
    backs = []
    for a in range(arrays):
        total = inputs[a][me].astype(jnp.float32)
        for k in range(1, n):
            total = total + landed[a][k - 1].astype(jnp.float32)
        reduced[a][...] = total.astype(reduced[a].dtype)
        for k in range(1, n):
            copy = pltpu.make_async_remote_copy(
                src_ref=reduced[a],
                dst_ref=whole[a].at[me],
                send_sem=sends_back.at[a, k - 1],
                recv_sem=arrivals_back.at[a, k - 1],
                device_id={axis: peers[k]},
                device_id_type=MESH,
            )
            copy.start()
            backs.append(copy)
        outputs[a][me] = reduced[a][...]
    for b in range(early, blocks):
        select_columns(b)
    for copy in copies:
        copy.wait_send()
    for copy in backs:
        copy.wait()
    for a in range(arrays):
        for k in range(1, n):
            outputs[a][peers[k]] = whole[a][peers[k]]


def sum_over(axis, n, collective_id, arrays, gather=None):
    cut = [a.reshape(n, a.shape[0] // n, a.shape[1]) for a in arrays]
    count = len(cut)
    vmem = pl.BlockSpec(memory_space=pltpu.VMEM)
    operands, in_specs = list(cut), [vmem] * count
    shapes = [jax.ShapeDtypeStruct(a.shape, a.dtype) for a in cut]
    scratch = [pltpu.VMEM((n - 1,) + a.shape[1:], a.dtype) for a in cut]
    scratch += [pltpu.VMEM(a.shape[1:], a.dtype) for a in cut]
    scratch += [pltpu.VMEM(a.shape, a.dtype) for a in cut]
    scratch += [pltpu.SemaphoreType.DMA((count, n - 1))] * 4
    plan = None
    if gather is not None:
        pool, picks, start, rows = gather
        block = 256 if rows % 256 == 0 else rows
        plan = (start, block, rows // block)
        operands += [pool, picks[None, :]]
        in_specs += [pl.BlockSpec(memory_space=pl.ANY), vmem]
        shapes.append(jax.ShapeDtypeStruct((rows, picks.shape[0]), pool.dtype))
        scratch += [
            pltpu.VMEM((rows, pool.shape[1]), pool.dtype),
            pltpu.VMEM((pool.shape[1], picks.shape[0]), pool.dtype),
            pltpu.SemaphoreType.DMA((rows // block,)),
        ]
    outs = pl.pallas_call(
        functools.partial(sum_kernel, axis, n, count, plan),
        out_shape=shapes,
        in_specs=in_specs,
        out_specs=[vmem] * len(shapes),
        scratch_shapes=scratch,
        compiler_params=pltpu.CompilerParams(
            collective_id=collective_id, has_side_effects=True,
            vmem_limit_bytes=48 * 1024 * 1024,
        ),
        name=f"sum_{axis}_{collective_id}",
    )(*operands)
    return [o.reshape(a.shape) for o, a in zip(outs, arrays)] + list(outs[count:])


def inverse_factor(gram):
    size = gram.shape[0]
    rows = lax.broadcasted_iota(jnp.int32, (size, size), 0)
    columns = lax.broadcasted_iota(jnp.int32, (size, size), 1)
    left = gram
    right = jnp.where(rows == columns, 1.0, 0.0).astype(jnp.float32)
    for k in range(size):
        scale = 1.0 / jnp.sqrt(left[k:k + 1, k:k + 1])
        column = jnp.where(rows[:, :1] > k, left[:, k:k + 1] * scale, 0.0)
        left_row = left[k:k + 1, :] * scale
        right_row = right[k:k + 1, :] * scale
        left = left - column * left_row
        right = jnp.where(rows == k, right_row, right - column * right_row)
    return right


def exact_product(left, right):
    return jnp.dot(
        left, right, precision=lax.Precision.HIGHEST, preferred_element_type=jnp.float32
    )


def normalise_kernel(gram_ref, stepped_ref, *refs):
    inverse = inverse_factor(gram_ref[...])
    if len(refs) == 1:
        refs[0][...] = exact_product(inverse, stepped_ref[...])
        return
    raw_ref, loadings_ref, scores_ref = refs
    scores_ref[...] = exact_product(inverse, raw_ref[...].astype(jnp.float32)).astype(
        scores_ref.dtype
    )
    loadings_ref[...] = exact_product(inverse, stepped_ref[...])


def normalise(gram, stepped, raw=None):
    shapes = [jax.ShapeDtypeStruct(stepped.shape, jnp.float32)]
    operands = [gram, stepped]
    if raw is not None:
        shapes.append(jax.ShapeDtypeStruct(raw.shape, jnp.bfloat16))
        operands.append(raw)
    return pl.pallas_call(
        normalise_kernel,
        out_shape=shapes,
        in_specs=[pl.BlockSpec(memory_space=pltpu.VMEM)] * len(operands),
        out_specs=[pl.BlockSpec(memory_space=pltpu.VMEM)] * len(shapes),
        name="normalise",
    )(*operands)


def select(pool, picks, start):
    ids = jnp.arange(pool.shape[1], dtype=jnp.int32)
    hot = (ids[:, None] == picks[None, :]).astype(pool.dtype)
    return jnp.dot(pool[start:], hot, preferred_element_type=jnp.float32).astype(pool.dtype)


def stacked(x):
    high = x.astype(jnp.bfloat16)
    rest = (x - high.astype(jnp.float32)).astype(jnp.bfloat16)
    return jnp.concatenate([high, rest], axis=0)


def folded(x):
    size = x.shape[0] // 2
    return x[:size] + x[size:]


def whitening(gram):
    size = gram.shape[0]
    rows = lax.broadcasted_iota(jnp.int32, (size, 2 * size), 0)
    columns = lax.broadcasted_iota(jnp.int32, (size, 2 * size), 1)
    state = jnp.concatenate([gram, jnp.zeros_like(gram)], axis=1)
    state = jnp.where(columns == rows + size, 1.0, state)
    for k in range(size):
        scale = lax.rsqrt(state[k:k + 1, k:k + 1])
        column = jnp.where(rows[:, :1] > k, state[:, k:k + 1] * scale, 0.0)
        row = state[k:k + 1, :] * scale
        state = jnp.where(rows == k, row, state - column * row)
    return state[:, size:]


def fused_kernel(
    genes, cells, steps, pool_hbm, picks_ref, init_ref, out_ref,
    pool, pool_t, hot, chosen, sums, mean, stepped, loadings, both, grams, scores, part, landed,
    low, spread, ahead, landed_core, mine, landed_pair, total,
    loaded, sums_send, sums_recv, gram_send, gram_recv, part_send, part_recv, low_send, low_recv,
    core_send, core_recv, pair_send, pair_recv, total_send, total_recv,
):
    me, group = lax.axis_index("gene"), lax.axis_index("cell")
    comps, local = stepped.shape
    local_pool, batch = hot.shape
    width = batch // genes
    block = 256
    half = local // 2
    pieces = half // block
    side = lax.rem(group, 2)
    other_side = 1 - side
    partner = group + 1 - 2 * side
    across = lax.rem(group + 2, cells)
    share = 1.0 / (batch * cells)
    peers = [lax.rem(me + k, genes) for k in range(genes)]
    sources = [lax.rem(me + genes - k, genes) for k in range(genes)]
    barrier = pltpu.get_barrier_semaphore()
    for k in range(1, genes):
        pl.semaphore_signal(barrier, inc=1, device_id={"gene": peers[k]}, device_id_type=MESH)
    for k in range(1, cells):
        pl.semaphore_signal(
            barrier, inc=1, device_id={"cell": lax.rem(group + k, cells)}, device_id_type=MESH
        )

    def load(b):
        rows = pl.ds(pl.multiple_of(b * block, block), block)
        return pltpu.make_async_copy(pool_hbm.at[rows], pool.at[rows], loaded.at[b])

    for b in range(local // block):
        load(b).start()

    def remote(src, dst, send, recv, where):
        return pltpu.make_async_remote_copy(
            src_ref=src, dst_ref=dst, send_sem=send, recv_sem=recv,
            device_id=where, device_id_type=MESH,
        )

    def span(i, size):
        return pl.ds(pl.multiple_of(i * size, 128), size)

    chosen[...] = jnp.zeros_like(chosen)

    for s in range(steps):
        ids = picks_ref[s:s + 1, :] - group * local_pool
        upper = lax.broadcasted_iota(jnp.int32, (local_pool // 128, batch), 0)
        lower = lax.broadcasted_iota(jnp.int32, (128, batch), 0)
        upper = jnp.where(upper == lax.shift_right_logical(ids, 7), 1.0, 0.0).astype(jnp.bfloat16)
        lower = jnp.where(lower == (ids & 127), 1.0, 0.0).astype(jnp.bfloat16)
        counts = transposed_product(upper, lower)
        for h in range(local_pool // 128):
            chosen[s:s + 1, h * 128:(h + 1) * 128] = counts[h:h + 1, :]

    def mark(s):
        ids = picks_ref[pl.ds(s, 1), :] - group * local_pool
        depth = 256

        def piece(i, carry):
            numbers = lax.broadcasted_iota(jnp.int32, (depth, batch), 0) + i * depth
            hot[span(i, depth), :] = jnp.where(numbers == ids, 1.0, 0.0).astype(hot.dtype)
            return carry

        lax.fori_loop(0, local_pool // depth, piece, 0)

    def turn(b, carry):
        load(b).wait()
        rows = span(b, block)
        unit = jnp.where(
            lax.broadcasted_iota(jnp.int32, (block, block), 0)
            == lax.broadcasted_iota(jnp.int32, (block, block), 1), 1.0, 0.0,
        ).astype(jnp.bfloat16)

        def piece(j, inner):
            pool_t[span(j, block), rows] = transposed_product(
                unit, pool[rows, span(j, block)]
            ).astype(pool_t.dtype)
            return inner

        lax.fori_loop(0, local_pool // block, piece, 0)
        sums[group, :, rows] = jnp.dot(
            chosen[...].astype(jnp.bfloat16), pool_t[:, rows], preferred_element_type=jnp.float32
        )
        return carry

    lax.fori_loop(0, local // block, turn, 0)
    pl.semaphore_wait(barrier, genes + cells - 2)
    sums_out = [
        remote(
            sums.at[group], sums.at[group], sums_send.at[k - 1], sums_recv.at[k - 1],
            {"cell": lax.rem(group + k, cells)},
        )
        for k in range(1, cells)
    ]
    for copy in sums_out:
        copy.start()
    mark(0)
    stepped[...] = init_ref[...]
    for copy in sums_out:
        copy.wait()
    whole = sums[0]
    for k in range(1, cells):
        whole = whole + sums[k]
    mean[...] = whole * share

    def gram_copies():
        return [
            remote(
                grams.at[me], grams.at[me], gram_send.at[k - 1], gram_recv.at[k - 1],
                {"gene": peers[k]},
            )
            for k in range(1, genes)
        ]

    def start_gram():
        both[...] = stacked(stepped[...])
        product = folded(transposed_product(both[...], both[...]))
        grams[me] = product[:, :comps] + product[:, comps:]
        for copy in gram_copies():
            copy.start()

    def finish_gram():
        for copy in gram_copies():
            copy.wait_recv()
        gram = grams[0]
        for k in range(1, genes):
            gram = gram + grams[k]
        return whitening(gram)

    def doubled(inverse):
        pair = stacked(inverse)
        return jnp.concatenate([pair, pair], axis=1)

    def step(s, carry):
        start_gram()
        mean_row = mean[pl.ds(s, 1), :]
        high = both[:comps, :]
        shift = jnp.sum(high.astype(jnp.float32) * mean_row, axis=1, keepdims=True)
        wide = 512

        def score(j, inner):
            columns = span(j, wide)
            product = jnp.dot(high, pool[:, columns], preferred_element_type=jnp.float32)
            scores[:, columns] = (product - shift).astype(scores.dtype)
            return inner

        lax.fori_loop(0, local_pool // wide, score, 0)
        outward = [
            remote(
                part.at[peers[k]], landed.at[me], part_send.at[k - 1], part_recv.at[k - 1],
                {"gene": peers[k]},
            )
            for k in range(1, genes)
        ]

        def narrow(j, inner):
            picked = jnp.dot(
                scores[...], hot[:, span(j, 2 * width)], preferred_element_type=jnp.float32
            ).astype(part.dtype)
            part[2 * j] = picked[:, :width]
            part[2 * j + 1] = picked[:, width:]
            return inner

        lax.fori_loop(0, genes // 2, narrow, 0)
        for copy in outward:
            copy.start()
        inverse = finish_gram()
        unit = jnp.where(
            lax.broadcasted_iota(jnp.int32, (comps, comps), 0)
            == lax.broadcasted_iota(jnp.int32, (comps, comps), 1), 1.0, 0.0,
        )
        factor = doubled(jnp.where(s == 0, unit, inverse))

        def apply(j, inner):
            columns = span(j, wide)
            loadings[:, columns] = folded(
                jnp.dot(factor, both[:, columns], preferred_element_type=jnp.float32)
            )
            return inner

        lax.fori_loop(0, local // wide, apply, 0)
        for copy in outward:
            copy.wait_recv()
        landed[me] = part[me]
        raw = landed[0].astype(jnp.float32)
        for k in range(1, genes):
            raw = raw + landed[k].astype(jnp.float32)
        own = span(me, width)
        low[:, own] = folded(
            jnp.dot(factor, stacked(raw), preferred_element_type=jnp.float32)
        ).astype(low.dtype)
        shared = [
            remote(
                low.at[:, own], low.at[:, own], low_send.at[k - 1], low_recv.at[k - 1],
                {"gene": peers[k]},
            )
            for k in range(1, genes)
        ]
        for copy in shared:
            copy.start()
        for copy in shared:
            copy.wait_recv()
        scores_low = low[...]
        row_totals = jnp.sum(scores_low.astype(jnp.float32), axis=1, keepdims=True)

        def widen(j, inner):
            rows = span(j, wide)
            spread[:, rows] = transposed_product(scores_low, hot[rows, :]).astype(spread.dtype)
            return inner

        lax.fori_loop(0, local_pool // wide, widen, 0)

        def partial(columns):
            raw_update = jnp.dot(
                spread[...], pool_t[:, columns], preferred_element_type=jnp.float32
            )
            return (raw_update - row_totals * mean[pl.ds(s, 1), columns]) * share

        def core_copy(j):
            columns = span(j, block)
            return remote(
                ahead.at[:, columns], landed_core.at[:, columns], core_send.at[j], core_recv.at[j],
                {"cell": partner},
            )

        slot = lax.rem(s, 2)

        def pair_copy(j):
            columns = span(j, block)
            return remote(
                mine.at[:, columns], landed_pair.at[slot, :, columns], pair_send.at[j],
                pair_recv.at[slot, j], {"cell": across},
            )

        def total_copy(j, which):
            columns = span(j, block)
            return remote(
                total.at[which, :, columns], total.at[which, :, columns], total_send.at[j],
                total_recv.at[j], {"cell": partner},
            )

        def give(j, inner):
            ahead[:, span(j, block)] = partial(
                pl.ds(pl.multiple_of(other_side * half + j * block, 128), block)
            ).astype(ahead.dtype)
            core_copy(j).start()
            return inner

        lax.fori_loop(0, pieces, give, 0)

        def take(j, inner):
            value = partial(pl.ds(pl.multiple_of(side * half + j * block, 128), block))
            core_copy(j).wait_recv()
            columns = span(j, block)
            mine[:, columns] = (
                value + landed_core[:, columns].astype(jnp.float32)
            ).astype(mine.dtype)
            pair_copy(j).start()
            return inner

        lax.fori_loop(0, pieces, take, 0)
        mark(jnp.minimum(s + 1, steps - 1))

        def join(j, inner):
            pair_copy(j).wait_recv()
            columns = span(j, block)
            value = mine[:, columns].astype(jnp.float32) + landed_pair[slot, :, columns].astype(
                jnp.float32
            )
            total[side, :, columns] = value
            total_copy(j, side).start()
            place = pl.ds(pl.multiple_of(side * half + j * block, 128), block)
            stepped[:, place] = loadings[:, place] + step_rate * value
            return inner

        lax.fori_loop(0, pieces, join, 0)

        def close(j, inner):
            total_copy(j, other_side).wait_recv()
            place = pl.ds(pl.multiple_of(other_side * half + j * block, 128), block)
            stepped[:, place] = (
                loadings[:, place] + step_rate * total[other_side, :, span(j, block)]
            )
            return inner

        lax.fori_loop(0, pieces, close, 0)

        def drain(j, inner):
            core_copy(j).wait_send()
            pair_copy(j).wait_send()
            total_copy(j, side).wait_send()
            return inner

        lax.fori_loop(0, pieces, drain, 0)
        for copy in gram_copies() + outward + shared:
            copy.wait_send()
        return carry

    lax.fori_loop(0, steps, step, 0)
    start_gram()
    factor = doubled(finish_gram() * math.sqrt(local * genes))

    def finish(j, carry):
        columns = span(j, 512)
        out_ref[:, columns] = folded(
            jnp.dot(factor, both[:, columns], preferred_element_type=jnp.float32)
        )
        return carry

    lax.fori_loop(0, local // 512, finish, 0)
    for copy in gram_copies():
        copy.wait_send()


def fits(genes, cells, pool_counts, cell_picks, loadings_init):
    batch = cell_picks.shape[1]
    return (
        cells == 4 and genes % 2 == 0 and batch == 128 * genes and cell_picks.shape[0] <= 8
        and pool_counts.shape[0] % 512 == 0 and pool_counts.shape[1] % 512 == 0
    )


def fused(genes, cells, pool_counts, cell_picks, loadings_init):
    local, local_pool = pool_counts.shape
    steps, batch = cell_picks.shape
    comps = loadings_init.shape[0]
    width = batch // genes
    half = local // 2
    pieces = half // 256
    low, full = jnp.bfloat16, jnp.float32
    vmem = pl.BlockSpec(memory_space=pltpu.VMEM)
    dma = pltpu.SemaphoreType.DMA
    return pl.pallas_call(
        functools.partial(fused_kernel, genes, cells, steps),
        out_shape=jax.ShapeDtypeStruct(loadings_init.shape, full),
        in_specs=[pl.BlockSpec(memory_space=pl.ANY), vmem, vmem],
        out_specs=vmem,
        scratch_shapes=[
            pltpu.VMEM((local, local_pool), low),
            pltpu.VMEM((local_pool, local), low),
            pltpu.VMEM((local_pool, batch), low),
            pltpu.VMEM((8, local_pool), full),
            pltpu.VMEM((cells, 8, local), full),
            pltpu.VMEM((8, local), full),
            pltpu.VMEM((comps, local), full),
            pltpu.VMEM((comps, local), full),
            pltpu.VMEM((2 * comps, local), low),
            pltpu.VMEM((genes, comps, comps), full),
            pltpu.VMEM((comps, local_pool), low),
            pltpu.VMEM((genes, comps, width), low),
            pltpu.VMEM((genes, comps, width), low),
            pltpu.VMEM((comps, batch), low),
            pltpu.VMEM((comps, local_pool), low),
            pltpu.VMEM((comps, half), low),
            pltpu.VMEM((comps, half), low),
            pltpu.VMEM((comps, half), low),
            pltpu.VMEM((2, comps, half), low),
            pltpu.VMEM((2, comps, half), full),
            dma((local // 256,)),
            dma((cells - 1,)), dma((cells - 1,)),
            dma((genes - 1,)), dma((genes - 1,)),
            dma((genes - 1,)), dma((genes - 1,)),
            dma((genes - 1,)), dma((genes - 1,)),
            dma((pieces,)), dma((pieces,)),
            dma((pieces,)), dma((2, pieces)),
            dma((pieces,)), dma((pieces,)),
        ],
        compiler_params=pltpu.CompilerParams(
            collective_id=8, has_side_effects=True, vmem_limit_bytes=66_000_000,
        ),
        name="fused_steps",
    )(pool_counts, cell_picks, loadings_init)


def shards(genes, cells, pool_counts, cell_picks, loadings_init):
    if fits(genes, cells, pool_counts, cell_picks, loadings_init):
        return fused(genes, cells, pool_counts, cell_picks, loadings_init)
    stepped = loadings_init
    local_pool = pool_counts.shape[1]
    group = lax.axis_index("cell")
    batch_total = cell_picks.shape[1] * cells
    local_genes = stepped.shape[1]
    gene_total = local_genes * genes
    picks = cell_picks - group * local_pool
    ids = jnp.arange(local_pool, dtype=jnp.int32)
    chosen = jnp.any(picks[:, :, None] == ids[None, None, :], axis=1).astype(jnp.bfloat16)
    sums = transposed_product(chosen, pool_counts)
    sums = jnp.pad(sums, ((0, -STEPS % cells), (0, 0)))
    split = local_genes // 2
    totals, upper = sum_over("cell", cells, 1, [sums], (pool_counts, picks[0], 0, split))
    lower = select(pool_counts, picks[0], split)
    means = totals / batch_total
    for s in range(STEPS):
        last = s == STEPS - 1
        mean = means[s]
        low = stepped.astype(jnp.bfloat16)
        product = jnp.dot(low[:, :split], upper, preferred_element_type=jnp.float32)
        product += jnp.dot(low[:, split:], lower, preferred_element_type=jnp.float32)
        shift = jnp.dot(low.astype(jnp.float32), mean, precision=lax.Precision.HIGHEST)
        part = (product - shift[:, None]).astype(jnp.bfloat16)
        ahead = None if last else (pool_counts, picks[s + 1], 0, split)
        if s == 0:
            scores_low, *next_upper = sum_over("gene", genes, 2, [part], ahead)
            loadings = stepped
        else:
            gram_part = jnp.dot(stepped, stepped.T, precision=lax.Precision.HIGHEST)
            raw, gram, *next_upper = sum_over(
                "gene", genes, 6 if last else 3, [part, gram_part], ahead
            )
            loadings, scores_low = normalise(gram, stepped, raw)
        raw_update = jnp.concatenate(
            [transposed_product(scores_low, upper), transposed_product(scores_low, lower)], axis=1
        )
        row_totals = jnp.sum(scores_low, axis=1, dtype=jnp.float32)
        local = (raw_update - row_totals[:, None] * mean[None, :]) / batch_total
        ahead = None if last else (pool_counts, picks[s + 1], split, local_genes - split)
        update, *next_lower = sum_over(
            "cell", cells, 7 if last else 4, [local.astype(jnp.bfloat16)], ahead
        )
        if not last:
            upper, lower = next_upper[0], next_lower[0]
        stepped = loadings + step_rate * update.astype(jnp.float32)
    gram_part = jnp.dot(stepped, stepped.T, precision=lax.Precision.HIGHEST)
    (gram,) = sum_over("gene", genes, 5, [gram_part])
    (loadings,) = normalise(gram, stepped)
    return loadings * math.sqrt(gene_total)


def solution(mesh):
    placed = (P("gene", "cell"), P(None, "cell"), P(None, "gene"))
    return jax.shard_map(
        functools.partial(shards, mesh.shape["gene"], mesh.shape["cell"]),
        mesh=mesh, in_specs=placed, out_specs=P(None, "gene"), check_vma=False,
    )
```

profile of v0, /device:TPU:0, one launch (start us, length us, event | category | flops | bytes accessed | tf_op | source)
XLA Modules:
  0.0 293.1 jit_solution(9485516009862712083)
XLA Ops:
  0.0 291.2 %fused_steps.1 = f32[64,2560]{1,0:T(8,128)} custom-call(bf16[2560,4096]{1,0:T(8,128)(2,1)} %pool_hbm.1, s32[7,1024]{1,0:T(8,128)} %picks_ref.1, f32[64,2560]{1,0:T(8,128)} %init_ref.1), custom_call_target="tpu_custom_call" | custom-call | tf_op jit(solution)/shard_map/fused_steps/pallas_call | solution.py:581
  291.2 2.0 copy.5
where the time goes:
time: 293 us
  Pallas kernels  291 us (99%)
    pallas_call x1, Pallas kernels, fused(): pl.pallas_call(functools.partial(fused_kernel, genes, cells, steps), out_...  291 us

commit v1 on v0

--- a/solution.py
+++ b/solution.py
@@ -230,31 +230,48 @@
 
 
 def whitening(gram):
-    size = gram.shape[0]
-    rows = lax.broadcasted_iota(jnp.int32, (size, 2 * size), 0)
-    columns = lax.broadcasted_iota(jnp.int32, (size, 2 * size), 1)
+    size, panel = gram.shape[0], 8
+    wide = 2 * size
+    rows = lax.broadcasted_iota(jnp.int32, (size, wide), 0)
+    columns = lax.broadcasted_iota(jnp.int32, (size, wide), 1)
     state = jnp.concatenate([gram, jnp.zeros_like(gram)], axis=1)
-    state = jnp.where(columns == rows + size, 1.0, state)
-    for k in range(size):
-        scale = lax.rsqrt(state[k:k + 1, k:k + 1])
-        column = jnp.where(rows[:, :1] > k, state[:, k:k + 1] * scale, 0.0)
-        row = state[k:k + 1, :] * scale
-        state = jnp.where(rows == k, row, state - column * row)
-    return state[:, size:]
+    rest = jnp.where(columns == rows + size, 1.0, state)
+    done = []
+    for first in range(0, size, panel):
+        height = size - first
+        local = rows[:height]
+        bands = [
+            jnp.broadcast_to(rest[:, first + j:first + j + 1], (height, wide))
+            for j in range(panel)
+        ]
+        top = rest[:panel]
+        below = rest[panel:]
+        for j in range(panel):
+            scale = lax.rsqrt(bands[j][j:j + 1, :])
+            column = jnp.where(local > j, bands[j] * scale, 0.0)
+            for i in range(j + 1, panel):
+                bands[i] = bands[i] - column * (bands[i][j:j + 1, :] * scale)
+            row = top[j:j + 1, :] * scale
+            top = jnp.where(local[:panel] == j, row, top - column[:panel] * row)
+            if height > panel:
+                below = below - column[panel:] * row
+        done.append(top)
+        rest = below
+    return jnp.concatenate(done, axis=0)[:, size:]
 
 
 def fused_kernel(
-    genes, cells, steps, pool_hbm, picks_ref, init_ref, out_ref,
-    pool, pool_t, hot, chosen, sums, mean, stepped, loadings, both, grams, scores, part, landed,
-    low, spread, ahead, landed_core, mine, landed_pair, total,
-    loaded, sums_send, sums_recv, gram_send, gram_recv, part_send, part_recv, low_send, low_recv,
-    core_send, core_recv, pair_send, pair_recv, total_send, total_recv,
+    genes, cells, steps, pool_hbm, picks_ref, lists_ref, init_hbm, out_hbm,
+    pool, pool_t, hot, hot_t, marks, chosen, sums, mean, loadings, both, gram_part, shifts, gathered,
+    gram_out, gram_in, grams, scores, part, landed, low, ahead, kept, landed_core, mine, landed_pair, total,
+    loaded, moved, sums_send, sums_recv, gram_send, gram_recv, share_send, share_recv, part_send, part_recv,
+    low_send, low_recv, core_send, core_recv, pair_send, pair_recv, total_send, total_recv,
 ):
     me, group = lax.axis_index("gene"), lax.axis_index("cell")
-    comps, local = stepped.shape
+    comps, local = loadings.shape
     local_pool, batch = hot.shape
     width = batch // genes
-    block = 256
+    block, wide = 256, 512
     half = local // 2
     pieces = half // block
     side = lax.rem(group, 2)
@@ -263,7 +280,6 @@
     across = lax.rem(group + 2, cells)
     share = 1.0 / (batch * cells)
     peers = [lax.rem(me + k, genes) for k in range(genes)]
-    sources = [lax.rem(me + genes - k, genes) for k in range(genes)]
     barrier = pltpu.get_barrier_semaphore()
     for k in range(1, genes):
         pl.semaphore_signal(barrier, inc=1, device_id={"gene": peers[k]}, device_id_type=MESH)
@@ -272,10 +288,16 @@
             barrier, inc=1, device_id={"cell": lax.rem(group + k, cells)}, device_id_type=MESH
         )
 
+    def span(i, size):
+        return pl.ds(pl.multiple_of(i * size, 128), size)
+
     def load(b):
-        rows = pl.ds(pl.multiple_of(b * block, block), block)
-        return pltpu.make_async_copy(pool_hbm.at[rows], pool.at[rows], loaded.at[b])
-
+        return pltpu.make_async_copy(
+            pool_hbm.at[span(b, block)], pool.at[span(b, block)], loaded.at[b]
+        )
+
+    take_init = pltpu.make_async_copy(init_hbm, loadings, moved.at[0])
+    take_init.start()
     for b in range(local // block):
         load(b).start()
 
@@ -285,11 +307,13 @@
             device_id=where, device_id_type=MESH,
         )
 
-    def span(i, size):
-        return pl.ds(pl.multiple_of(i * size, 128), size)
+    def equal_mask(size):
+        return (
+            lax.broadcasted_iota(jnp.int32, (size, size), 0)
+            == lax.broadcasted_iota(jnp.int32, (size, size), 1)
+        )
 
     chosen[...] = jnp.zeros_like(chosen)
-
     for s in range(steps):
         ids = picks_ref[s:s + 1, :] - group * local_pool
         upper = lax.broadcasted_iota(jnp.int32, (local_pool // 128, batch), 0)
@@ -302,36 +326,69 @@
 
     def mark(s):
         ids = picks_ref[pl.ds(s, 1), :] - group * local_pool
-        depth = 256
-
-        def piece(i, carry):
-            numbers = lax.broadcasted_iota(jnp.int32, (depth, batch), 0) + i * depth
-            hot[span(i, depth), :] = jnp.where(numbers == ids, 1.0, 0.0).astype(hot.dtype)
-            return carry
-
-        lax.fori_loop(0, local_pool // depth, piece, 0)
-
-    def turn(b, carry):
+        numbers = lax.broadcasted_iota(jnp.int32, (128, batch), 0)
+        marks[...] = jnp.where(numbers == (ids & 127), 1.0, 0.0).astype(marks.dtype)
+        tiles = jnp.broadcast_to(
+            lax.shift_right_logical(ids, 7).astype(jnp.float32), (16, batch)
+        ).astype(jnp.bfloat16)
+        for i in range(local_pool // 128):
+            here = tiles == jnp.bfloat16(i)
+            for k in range(8):
+                rows = slice(k * 16, (k + 1) * 16)
+                hot[i * 128 + k * 16:i * 128 + (k + 1) * 16, :] = jnp.where(
+                    here, marks[rows, :], jnp.bfloat16(0)
+                )
+
+    def mark_turned(s):
+        ids = lists_ref[s] - group * local_pool
+        upper = lax.shift_right_logical(ids, 7).astype(jnp.float32).T
+        lower = (ids & 127).astype(jnp.float32).T
+        lanes = lax.broadcasted_iota(jnp.int32, (128, 128), 1).astype(jnp.float32)
+        for h in range(batch // 128):
+            found = jnp.where(
+                lanes == jnp.broadcast_to(lower[:, h:h + 1], (128, 128)), 1.0, 0.0
+            ).astype(jnp.bfloat16)
+            tiles = jnp.broadcast_to(upper[:, h:h + 1], (128, 128)).astype(jnp.bfloat16)
+            for i in range(local_pool // 128):
+                hot_t[h * 128:(h + 1) * 128, i * 128:(i + 1) * 128] = jnp.where(
+                    tiles == jnp.bfloat16(i), found, jnp.bfloat16(0)
+                )
+
+    def absorb(*arrived, fresh=False):
+        highs = []
+        product = 0.0 if fresh else gram_part[...]
+        for place, value in arrived:
+            pair = stacked(value)
+            both[:, place] = pair
+            highs.append(pair[:comps])
+            product = product + transposed_product(pair, pair)
+        gram_part[...] = product
+        for j in range(local_pool // wide):
+            columns = slice(j * wide, (j + 1) * wide)
+            product = sum(
+                jnp.dot(high, pool[place, columns], preferred_element_type=jnp.float32)
+                for high, (place, _) in zip(highs, arrived)
+            )
+            gathered[:, columns] = product if fresh else gathered[:, columns] + product
+
+    def note_shift(place, s):
+        value = both[:comps, place].astype(jnp.float32) * mean[pl.ds(s, 1), place]
+        shifts[...] = shifts[...] + value[:, :128] + value[:, 128:]
+
+    gram_part[...] = jnp.zeros_like(gram_part)
+    shifts[...] = jnp.zeros_like(shifts)
+    gathered[...] = jnp.zeros_like(gathered)
+    take_init.wait()
+    chosen_low = chosen[...].astype(jnp.bfloat16)
+
+    def read(b, carry):
         load(b).wait()
         rows = span(b, block)
-        unit = jnp.where(
-            lax.broadcasted_iota(jnp.int32, (block, block), 0)
-            == lax.broadcasted_iota(jnp.int32, (block, block), 1), 1.0, 0.0,
-        ).astype(jnp.bfloat16)
-
-        def piece(j, inner):
-            pool_t[span(j, block), rows] = transposed_product(
-                unit, pool[rows, span(j, block)]
-            ).astype(pool_t.dtype)
-            return inner
-
-        lax.fori_loop(0, local_pool // block, piece, 0)
-        sums[group, :, rows] = jnp.dot(
-            chosen[...].astype(jnp.bfloat16), pool_t[:, rows], preferred_element_type=jnp.float32
-        )
+        sums[group, :, rows] = transposed_product(chosen_low, pool[rows, :])
+        absorb((rows, loadings[:, rows]))
         return carry
 
-    lax.fori_loop(0, local // block, turn, 0)
+    lax.fori_loop(0, local // block, read, 0)
     pl.semaphore_wait(barrier, genes + cells - 2)
     sums_out = [
         remote(
@@ -342,8 +399,70 @@
     ]
     for copy in sums_out:
         copy.start()
+
+    def gram_copies():
+        return [
+            remote(
+                gram_out.at[peers[k]], gram_in.at[me], gram_send.at[k - 1], gram_recv.at[k - 1],
+                {"gene": peers[k]},
+            )
+            for k in range(1, genes)
+        ]
+
+    def gram_shares():
+        return [
+            remote(
+                grams.at[me], grams.at[me], share_send.at[k - 1], share_recv.at[k - 1],
+                {"gene": peers[k]},
+            )
+            for k in range(1, genes)
+        ]
+
+    def start_gram():
+        product = folded(gram_part[...])
+        product = product[:, :comps] + product[:, comps:]
+        packed = jnp.concatenate([product[:comps // 2], product[comps // 2:]], axis=1)
+        height = gram_out.shape[1]
+        for k in range(genes):
+            gram_out[k] = packed[k * height:(k + 1) * height]
+        for copy in gram_copies():
+            copy.start()
+
+    def share_gram():
+        for copy in gram_copies():
+            copy.wait_recv()
+        gram_in[me] = gram_out[me]
+        gram = gram_in[0]
+        for k in range(1, genes):
+            gram = gram + gram_in[k]
+        grams[me] = gram
+        for copy in gram_shares():
+            copy.start()
+
+    def finish_gram():
+        for copy in gram_shares():
+            copy.wait_recv()
+        gram = jnp.concatenate([grams[k] for k in range(genes)], axis=0)
+        return whitening(jnp.concatenate([gram[:, :comps], gram[:, comps:]], axis=0))
+
+    def doubled(inverse):
+        pair = stacked(inverse)
+        return jnp.concatenate([pair, pair], axis=1)
+
+    unit = jnp.where(equal_mask(block), 1.0, 0.0).astype(jnp.bfloat16)
+
+    def turn(b, carry):
+        rows = span(b, block)
+
+        for j in range(local_pool // block):
+            cells_here = slice(j * block, (j + 1) * block)
+            pool_t[cells_here, rows] = transposed_product(
+                unit, pool[rows, cells_here]
+            ).astype(pool_t.dtype)
+        return carry
+
+    lax.fori_loop(0, local // block, turn, 0)
     mark(0)
-    stepped[...] = init_ref[...]
     for copy in sums_out:
         copy.wait()
     whole = sums[0]
@@ -351,92 +470,58 @@
         whole = whole + sums[k]
     mean[...] = whole * share
 
-    def gram_copies():
-        return [
-            remote(
-                grams.at[me], grams.at[me], gram_send.at[k - 1], gram_recv.at[k - 1],
-                {"gene": peers[k]},
-            )
-            for k in range(1, genes)
-        ]
-
-    def start_gram():
-        both[...] = stacked(stepped[...])
-        product = folded(transposed_product(both[...], both[...]))
-        grams[me] = product[:, :comps] + product[:, comps:]
-        for copy in gram_copies():
-            copy.start()
-
-    def finish_gram():
-        for copy in gram_copies():
-            copy.wait_recv()
-        gram = grams[0]
-        for k in range(1, genes):
-            gram = gram + grams[k]
-        return whitening(gram)
-
-    def doubled(inverse):
-        pair = stacked(inverse)
-        return jnp.concatenate([pair, pair], axis=1)
+    def first_shift(b, carry):
+        note_shift(span(b, block), 0)
+        return carry
+
+    lax.fori_loop(0, local // block, first_shift, 0)
+
+    def total_copy(j, which):
+        columns = span(j, block)
+        return remote(
+            total.at[which, :, columns], total.at[which, :, columns], total_send.at[j],
+            total_recv.at[j], {"cell": partner},
+        )
+
+    def part_copy(peer):
+        return remote(
+            part.at[peer], landed.at[me], part_send.at[peer], part_recv.at[me], {"gene": peer}
+        )
+
+    def arrival(source):
+        return remote(
+            part.at[source], landed.at[source], part_send.at[source], part_recv.at[source],
+            {"gene": source},
+        )
 
     def step(s, carry):
         start_gram()
-        mean_row = mean[pl.ds(s, 1), :]
-        high = both[:comps, :]
-        shift = jnp.sum(high.astype(jnp.float32) * mean_row, axis=1, keepdims=True)
-        wide = 512
-
-        def score(j, inner):
-            columns = span(j, wide)
-            product = jnp.dot(high, pool[:, columns], preferred_element_type=jnp.float32)
-            scores[:, columns] = (product - shift).astype(scores.dtype)
-            return inner
-
-        lax.fori_loop(0, local_pool // wide, score, 0)
-        outward = [
-            remote(
-                part.at[peers[k]], landed.at[me], part_send.at[k - 1], part_recv.at[k - 1],
-                {"gene": peers[k]},
-            )
-            for k in range(1, genes)
-        ]
-
-        def narrow(j, inner):
-            picked = jnp.dot(
-                scores[...], hot[:, span(j, 2 * width)], preferred_element_type=jnp.float32
-            ).astype(part.dtype)
-            part[2 * j] = picked[:, :width]
-            part[2 * j + 1] = picked[:, width:]
-            return inner
-
-        lax.fori_loop(0, genes // 2, narrow, 0)
-        for copy in outward:
-            copy.start()
-        inverse = finish_gram()
-        unit = jnp.where(
-            lax.broadcasted_iota(jnp.int32, (comps, comps), 0)
-            == lax.broadcasted_iota(jnp.int32, (comps, comps), 1), 1.0, 0.0,
-        )
-        factor = doubled(jnp.where(s == 0, unit, inverse))
-
-        def apply(j, inner):
-            columns = span(j, wide)
-            loadings[:, columns] = folded(
-                jnp.dot(factor, both[:, columns], preferred_element_type=jnp.float32)
-            )
-            return inner
-
-        lax.fori_loop(0, local // wide, apply, 0)
-        for copy in outward:
-            copy.wait_recv()
+        shift = jnp.sum(shifts[...], axis=1, keepdims=True)
+        scores[...] = (gathered[...] - shift).astype(scores.dtype)
+
+        pairs = [lax.rem(j + me // 2 + 1, genes // 2) for j in range(genes // 2)]
+        for first in range(0, genes // 2, 2):
+            for pair in pairs[first:first + 2]:
+                picked = jnp.dot(
+                    scores[...], hot[:, span(pair, 2 * width)], preferred_element_type=jnp.float32
+                ).astype(part.dtype)
+                for k in range(2):
+                    part[2 * pair + k] = picked[:, k * width:(k + 1) * width]
+            for j in range(first, min(first + 2, genes // 2)):
+                if j < genes // 2 - 1:
+                    part_copy(2 * pairs[j]).start()
+                    part_copy(2 * pairs[j] + 1).start()
+                else:
+                    part_copy(me + 1 - 2 * lax.rem(me, 2)).start()
+        share_gram()
+        for k in range(1, genes):
+            arrival(peers[k]).wait_recv()
         landed[me] = part[me]
         raw = landed[0].astype(jnp.float32)
         for k in range(1, genes):
             raw = raw + landed[k].astype(jnp.float32)
         own = span(me, width)
-        low[:, own] = folded(
-            jnp.dot(factor, stacked(raw), preferred_element_type=jnp.float32)
-        ).astype(low.dtype)
+        low[:, own] = raw.astype(low.dtype)
         shared = [
             remote(
                 low.at[:, own], low.at[:, own], low_send.at[k - 1], low_recv.at[k - 1],
@@ -446,21 +531,45 @@
         ]
         for copy in shared:
             copy.start()
+
+        mark_turned(s)
+        inverse = finish_gram()
+        pair = stacked(jnp.where(s == 0, jnp.where(equal_mask(comps), 1.0, 0.0), inverse))
+        factor = jnp.concatenate([pair, pair], axis=1)
+        for j in range(local // wide):
+            columns = slice(j * wide, (j + 1) * wide)
+            loadings[:, columns] = folded(
+                jnp.dot(factor, both[:, columns], preferred_element_type=jnp.float32)
+            )
+        for copy in gram_copies() + gram_shares():
+            copy.wait_send()
+        for k in range(1, genes):
+            part_copy(peers[k]).wait_send()
+
+        @pl.when(s > 0)
+        def _():
+            for j in range(pieces):
+                total_copy(j, side).wait_send()
+
         for copy in shared:
             copy.wait_recv()
-        scores_low = low[...]
+        scores_low = folded(
+            jnp.dot(pair, low[...], preferred_element_type=jnp.float32)
+        ).astype(low.dtype)
         row_totals = jnp.sum(scores_low.astype(jnp.float32), axis=1, keepdims=True)
 
-        def widen(j, inner):
-            rows = span(j, wide)
-            spread[:, rows] = transposed_product(scores_low, hot[rows, :]).astype(spread.dtype)
-            return inner
-
-        lax.fori_loop(0, local_pool // wide, widen, 0)
+        for j in range(local_pool // wide):
+            columns = slice(j * wide, (j + 1) * wide)
+            scores[:, columns] = jnp.dot(
+                scores_low, hot_t[:, columns], preferred_element_type=jnp.float32
+            ).astype(scores.dtype)
+
+        def place_of(which, j):
+            return pl.ds(pl.multiple_of(which * half + j * block, 128), block)
 
         def partial(columns):
             raw_update = jnp.dot(
-                spread[...], pool_t[:, columns], preferred_element_type=jnp.float32
+                scores[...], pool_t[:, columns], preferred_element_type=jnp.float32
             )
             return (raw_update - row_totals * mean[pl.ds(s, 1), columns]) * share
 
@@ -480,36 +589,40 @@
                 pair_recv.at[slot, j], {"cell": across},
             )
 
-        def total_copy(j, which):
-            columns = span(j, block)
-            return remote(
-                total.at[which, :, columns], total.at[which, :, columns], total_send.at[j],
-                total_recv.at[j], {"cell": partner},
-            )
-
-        def give(j, inner):
-            ahead[:, span(j, block)] = partial(
-                pl.ds(pl.multiple_of(other_side * half + j * block, 128), block)
-            ).astype(ahead.dtype)
-            core_copy(j).start()
-            return inner
-
-        lax.fori_loop(0, pieces, give, 0)
-
-        def take(j, inner):
-            value = partial(pl.ds(pl.multiple_of(side * half + j * block, 128), block))
+        def take(j):
             core_copy(j).wait_recv()
             columns = span(j, block)
             mine[:, columns] = (
-                value + landed_core[:, columns].astype(jnp.float32)
+                kept[:, columns] + landed_core[:, columns].astype(jnp.float32)
             ).astype(mine.dtype)
             pair_copy(j).start()
-            return inner
-
-        lax.fori_loop(0, pieces, take, 0)
-        mark(jnp.minimum(s + 1, steps - 1))
-
-        def join(j, inner):
+
+        def give(places):
+            for j in places:
+                ahead[:, span(j, block)] = partial(place_of(other_side, j)).astype(ahead.dtype)
+
+        def keep(places):
+            for j in places:
+                kept[:, span(j, block)] = partial(place_of(side, j))
+
+        early = min(2, pieces)
+        give(range(early))
+        for j in range(early):
+            core_copy(j).start()
+        give(range(early, pieces))
+        keep(range(1))
+        for j in range(early, pieces):
+            core_copy(j).start()
+        take(0)
+        for first in range(1, pieces, 2):
+            together = range(first, min(first + 2, pieces))
+            keep(together)
+            for j in together:
+                take(j)
+        later = jnp.minimum(s + 1, steps - 1)
+        mark(later)
+
+        def join(j):
             pair_copy(j).wait_recv()
             columns = span(j, block)
             value = mine[:, columns].astype(jnp.float32) + landed_pair[slot, :, columns].astype(
@@ -517,54 +630,66 @@
             )
             total[side, :, columns] = value
             total_copy(j, side).start()
-            place = pl.ds(pl.multiple_of(side * half + j * block, 128), block)
-            stepped[:, place] = loadings[:, place] + step_rate * value
-            return inner
-
-        lax.fori_loop(0, pieces, join, 0)
-
-        def close(j, inner):
+            place = place_of(side, j)
+            return place, loadings[:, place] + step_rate * value
+
+        def close(j):
             total_copy(j, other_side).wait_recv()
-            place = pl.ds(pl.multiple_of(other_side * half + j * block, 128), block)
-            stepped[:, place] = (
-                loadings[:, place] + step_rate * total[other_side, :, span(j, block)]
-            )
-            return inner
-
-        lax.fori_loop(0, pieces, close, 0)
-
-        def drain(j, inner):
+            place = place_of(other_side, j)
+            return place, loadings[:, place] + step_rate * total[other_side, :, span(j, block)]
+
+        def settle_in(*arrived, fresh=False):
+            absorb(*arrived, fresh=fresh)
+            if fresh:
+                shifts[...] = jnp.zeros_like(shifts)
+            for place, _ in arrived:
+                note_shift(place, later)
+
+        before = []
+        for first in range(0, pieces, 2):
+            now = range(first, min(first + 2, pieces))
+            settle_in(*[join(j) for j in now], *[close(j) for j in before], fresh=first == 0)
+            before = now
+        settle_in(*[close(j) for j in before])
+        for j in range(pieces):
             core_copy(j).wait_send()
             pair_copy(j).wait_send()
-            total_copy(j, side).wait_send()
-            return inner
-
-        lax.fori_loop(0, pieces, drain, 0)
-        for copy in gram_copies() + outward + shared:
+        for copy in shared:
             copy.wait_send()
         return carry
 
     lax.fori_loop(0, steps, step, 0)
     start_gram()
+    share_gram()
     factor = doubled(finish_gram() * math.sqrt(local * genes))
 
+    def give_out(j):
+        return pltpu.make_async_copy(
+            loadings.at[:, span(j, wide)], out_hbm.at[:, span(j, wide)], moved.at[1 + j]
+        )
+
     def finish(j, carry):
-        columns = span(j, 512)
-        out_ref[:, columns] = folded(
+        columns = span(j, wide)
+        loadings[:, columns] = folded(
             jnp.dot(factor, both[:, columns], preferred_element_type=jnp.float32)
         )
+        give_out(j).start()
         return carry
 
-    lax.fori_loop(0, local // 512, finish, 0)
-    for copy in gram_copies():
+    lax.fori_loop(0, local // wide, finish, 0)
+    for j in range(local // wide):
+        give_out(j).wait()
+    for copy in gram_copies() + gram_shares():
         copy.wait_send()
+    for j in range(pieces):
+        total_copy(j, side).wait_send()
 
 
 def fits(genes, cells, pool_counts, cell_picks, loadings_init):
     batch = cell_picks.shape[1]
     return (
         cells == 4 and genes % 2 == 0 and batch == 128 * genes and cell_picks.shape[0] <= 8
-        and pool_counts.shape[0] % 512 == 0 and pool_counts.shape[1] % 512 == 0
+        and pool_counts.shape[0] % 512 == 0 and pool_counts.shape[1] % 1024 == 0
     )
 
 
@@ -576,48 +701,55 @@
     half = local // 2
     pieces = half // 256
     low, full = jnp.bfloat16, jnp.float32
-    vmem = pl.BlockSpec(memory_space=pltpu.VMEM)
+    vmem, anywhere = pl.BlockSpec(memory_space=pltpu.VMEM), pl.BlockSpec(memory_space=pl.ANY)
     dma = pltpu.SemaphoreType.DMA
     return pl.pallas_call(
         functools.partial(fused_kernel, genes, cells, steps),
         out_shape=jax.ShapeDtypeStruct(loadings_init.shape, full),
-        in_specs=[pl.BlockSpec(memory_space=pl.ANY), vmem, vmem],
-        out_specs=vmem,
+        in_specs=[anywhere, vmem, vmem, anywhere],
+        out_specs=anywhere,
         scratch_shapes=[
             pltpu.VMEM((local, local_pool), low),
             pltpu.VMEM((local_pool, local), low),
             pltpu.VMEM((local_pool, batch), low),
+            pltpu.VMEM((batch, local_pool), low),
+            pltpu.VMEM((128, batch), low),
             pltpu.VMEM((8, local_pool), full),
             pltpu.VMEM((cells, 8, local), full),
             pltpu.VMEM((8, local), full),
             pltpu.VMEM((comps, local), full),
-            pltpu.VMEM((comps, local), full),
             pltpu.VMEM((2 * comps, local), low),
-            pltpu.VMEM((genes, comps, comps), full),
+            pltpu.VMEM((2 * comps, 2 * comps), full),
+            pltpu.VMEM((comps, 128), full),
+            pltpu.VMEM((comps, local_pool), full),
+            pltpu.VMEM((genes, comps // 2 // genes, 2 * comps), full),
+            pltpu.VMEM((genes, comps // 2 // genes, 2 * comps), full),
+            pltpu.VMEM((genes, comps // 2 // genes, 2 * comps), full),
             pltpu.VMEM((comps, local_pool), low),
             pltpu.VMEM((genes, comps, width), low),
             pltpu.VMEM((genes, comps, width), low),
             pltpu.VMEM((comps, batch), low),
-            pltpu.VMEM((comps, local_pool), low),
             pltpu.VMEM((comps, half), low),
+            pltpu.VMEM((comps, half), full),
             pltpu.VMEM((comps, half), low),
             pltpu.VMEM((comps, half), low),
             pltpu.VMEM((2, comps, half), low),
             pltpu.VMEM((2, comps, half), full),
-            dma((local // 256,)),
+            dma((local // 256,)), dma((1 + local // 512,)),
             dma((cells - 1,)), dma((cells - 1,)),
             dma((genes - 1,)), dma((genes - 1,)),
             dma((genes - 1,)), dma((genes - 1,)),
+            dma((genes,)), dma((genes,)),
             dma((genes - 1,)), dma((genes - 1,)),
             dma((pieces,)), dma((pieces,)),
             dma((pieces,)), dma((2, pieces)),
             dma((pieces,)), dma((pieces,)),
         ],
         compiler_params=pltpu.CompilerParams(
-            collective_id=8, has_side_effects=True, vmem_limit_bytes=66_000_000,
+            collective_id=8, has_side_effects=True, vmem_limit_bytes=67_000_000,
         ),
         name="fused_steps",
-    )(pool_counts, cell_picks, loadings_init)
+    )(pool_counts, cell_picks, cell_picks.reshape(steps, batch // 128, 128), loadings_init)
 
 
 def shards(genes, cells, pool_counts, cell_picks, loadings_init):

time: 293 us -> 207 us (0.71)
  Pallas kernels: 291 us -> 204 us
    pallas_call x1, Pallas kernels: 291 us -> 204 us  [fused(): pl.pallas_call(functools.partial(fused_kernel, genes, cells, steps), out_...]
where the time goes in v1:
time: 207 us
  Pallas kernels  204 us (99%)
  local copies, waits for them, and re-layouts  3.34 us (2%)
    pallas_call x1, Pallas kernels, fused(): pl.pallas_call(functools.partial(fused_kernel, genes, cells, steps), out_...  204 us

profile of v1, /device:TPU:0, one launch (start us, length us, event | category | flops | bytes accessed | tf_op | source)
XLA Modules:
  0.0 207.2 jit_solution(9287767568449067757)
XLA Ops:
  0.0 1.4 copy.6
  1.4 203.8 %fused_steps.1 = f32[64,2560]{1,0:T(8,128)} custom-call(bf16[2560,4096]{1,0:T(8,128)(2,1)} %pool_hbm.1, s32[7,1024]{1,0:T(8,128)} %picks_ref.1, s32[7,8,128]{2,1,0:T(8,128)} %bitcast.5, f32[64,2560]{1,0:T(8,128)} %init_hbm.1), custom_call_target="tpu_custom_call" | custom-call | tf_op jit(solution)/shard_map/fused_steps/pallas_call | solution.py:706
  205.2 2.0 copy.8
